TPU v7x, 32 devices: a whole 2x2x4 slice. The times are simulated.
32 devices in a mesh: task: 2 (over x), ctx: 16 (over z, y, core).
Axes of the slice: x: 2, y: 2, z: 4, core: 2. Of those that a mesh axis runs over, the one named last changes fastest.
Arguments:
- base_queries: bfloat16 [2, 2048, 2048], P('task', 'ctx'), may hold values from -48 to 48
- adapter_input: bfloat16 [2, 2048, 16], P('task', 'ctx'), may hold values from -6 to 6
- adapter_up_weight: bfloat16 [2, 16, 2048], P('task'), may hold values from -1.5 to 1.5
- projected_keys: bfloat16 [2, 2048, 512], P('task', 'ctx'), may hold values from -6 to 6
- projected_values: bfloat16 [2, 2048, 512], P('task', 'ctx'), may hold values from -6 to 6
- output_gradient: bfloat16 [2, 2048, 2048], P('task', 'ctx'), may hold values from -0.52734375 to 0.52734375
- segments: int32 [2, 2048], P('task', 'ctx'), may hold values from 0 to 4, never falling along the last dimension, each value on 1 to 768 neighbouring positions
- solution: float32 [2, 32768], P('task'), may hold values from -1.5 to 1.5
- residual: float32 [2, 32768], P('task'), may hold values from -1.5 to 1.5
- direction: float32 [2, 32768], P('task'), may hold values from -1.5 to 1.5
- damping: float32 [2], P('task'), may hold values from 2 to 8
Outputs:
- new_solution: float32 [2, 32768], P('task', 'ctx')
- new_residual: float32 [2, 32768], P('task', 'ctx')
- new_direction: float32 [2, 32768], P('task', 'ctx')
- meta_gradient: float32 [32768], P('ctx')
Inputs may be any that keep to these rules, and one draw needn't show every extreme that they name: `segments`: segment numbers never fall along a task's tokens; each document holds 1 to 768 tokens, and some document holds exactly 768.
All inputs are finite; a program needn't handle non-finite values.
Results may differ from a plain program's by a relative error of at most 0.0073.
Values may be sent and summed in bfloat16 or wider, within the bound.
A program may use at most 64 MiB of HBM per device.

v0:
```python
import jax
import jax.numpy as jnp
from jax import lax
from jax.sharding import PartitionSpec as P

HEADS = 16
KV_HEADS = 4
HEAD_DIM = 128
ADAPTER_RANK = 16
SPAN = 6


def passed_along(value, axis, steps):
    count = lax.axis_size(axis)
    leading, last = (max(0, -steps), min(count, count - steps))
    return lax.ppermute(value, axis, [(source, source + steps) for source in range(leading, last)])


def attend(query_matrix, tangent_vectors, grads_in, key_window, value_window, allowed):
    per_group = HEADS // KV_HEADS
    score_scale = HEAD_DIM ** (-0.5)
    row_count = query_matrix.shape[0]
    head_parts = []
    for kv_index in range(KV_HEADS):
        low_col = kv_index * per_group * HEAD_DIM
        high_col = low_col + per_group * HEAD_DIM
        query_head = query_matrix[:, low_col:high_col].reshape(row_count, per_group, HEAD_DIM)
        tangent_head = tangent_vectors[:, low_col:high_col].reshape(row_count, per_group, HEAD_DIM)
        grad_head = grads_in[:, low_col:high_col].reshape(row_count, per_group, HEAD_DIM)
        key_head = key_window[:, kv_index * HEAD_DIM : (kv_index + 1) * HEAD_DIM]
        value_head = value_window[:, kv_index * HEAD_DIM : (kv_index + 1) * HEAD_DIM]
        scores = (
            jnp.einsum("tgd,kd->tgk", query_head, key_head, preferred_element_type=jnp.float32)
            * score_scale
        )
        slopes = (
            jnp.einsum("tgd,kd->tgk", tangent_head, key_head, preferred_element_type=jnp.float32)
            * score_scale
        )
        pulls = jnp.einsum("tgd,kd->tgk", grad_head, value_head, preferred_element_type=jnp.float32)
        key_mask = allowed[:, None, :]
        masked = jnp.where(key_mask, scores, -1e30)
        row_max = jnp.max(masked, axis=2, keepdims=True)
        exp_terms = jnp.exp(masked - row_max)
        probability = exp_terms / jnp.sum(exp_terms, axis=2, keepdims=True)
        mean_slope = jnp.sum(probability * slopes, axis=2, keepdims=True)
        mean_pull = jnp.sum(probability * pulls, axis=2, keepdims=True)
        centred = (slopes - mean_slope) * (pulls - mean_pull)
        covariance = jnp.sum(probability * centred, axis=2, keepdims=True)
        coef_rounded = (probability * (centred - covariance)).astype(jnp.bfloat16)
        head_rows = (
            jnp.einsum("tgk,kd->tgd", coef_rounded, key_head, preferred_element_type=jnp.float32)
            * score_scale
        )
        head_parts.append(head_rows.reshape(row_count, per_group * HEAD_DIM))
    return jnp.concatenate(head_parts, axis=1)


def per_device(
    base_queries,
    adapter_input,
    adapter_up_weight,
    projected_keys,
    projected_values,
    output_gradient,
    segments,
    solution,
    residual,
    direction,
    damping,
):
    tok_count = base_queries.shape[1]
    dev_index = lax.axis_index("ctx")
    adapter_rows = adapter_input[0]
    query_matrix = (
        base_queries[0].astype(jnp.float32)
        + jnp.dot(adapter_rows, adapter_up_weight[0], preferred_element_type=jnp.float32)
    ).astype(jnp.bfloat16)
    shift_matrix_fn = direction[0].reshape(ADAPTER_RANK, HEADS * HEAD_DIM)
    tangent_vectors = jnp.dot(
        adapter_rows.astype(jnp.float32), shift_matrix_fn, precision=lax.Precision.HIGHEST
    ).astype(jnp.bfloat16)
    own_block = (projected_keys[0], projected_values[0], segments[0])
    earlier = []
    for offset in range(1, SPAN + 1):
        earlier.append(passed_along((own_block[0], own_block[1], own_block[2]), "ctx", offset))
    ordered = earlier[::-1] + [own_block]
    key_window = jnp.concatenate([piece[0] for piece in ordered], axis=0)
    value_window = jnp.concatenate([piece[1] for piece in ordered], axis=0)
    seg_window = jnp.concatenate([piece[2] for piece in ordered], axis=0)
    window = (SPAN + 1) * tok_count
    key_place = dev_index * tok_count - SPAN * tok_count + jnp.arange(window, dtype=jnp.int32)
    query_place = dev_index * tok_count + jnp.arange(tok_count, dtype=jnp.int32)
    allowed = (
        (key_place[None, :] <= query_place[:, None])
        & (key_place[None, :] >= 0)
        & (seg_window[None, :] == segments[0][:, None])
    )
    curvature_product_rows = attend(
        query_matrix, tangent_vectors, output_gradient[0], key_window, value_window, allowed
    ).astype(jnp.bfloat16)
    curvature_product_term = jnp.dot(
        adapter_rows.T, curvature_product_rows, preferred_element_type=jnp.float32
    ).reshape(-1)
    damp_val = damping[0]
    dir_full = direction[0]
    res_full = residual[0]
    old_norm = jnp.sum(res_full * res_full)
    part_size = curvature_product_term.shape[0] // lax.axis_size("ctx")
    part_start = dev_index * part_size
    dir_part = lax.dynamic_slice_in_dim(dir_full, part_start, part_size, 0)
    sol_part = lax.dynamic_slice_in_dim(solution[0], part_start, part_size, 0)
    complete_curvature_product = lax.psum(curvature_product_term, "ctx")
    curved = dir_full + complete_curvature_product / damp_val
    step_len = old_norm / jnp.sum(dir_full * curved)
    res_next = res_full - step_len * curved
    ratio = jnp.sum(res_next * res_next) / old_norm
    new_residual = lax.dynamic_slice_in_dim(res_next, part_start, part_size, 0)
    new_direction = new_residual + ratio * dir_part
    new_solution = sol_part + step_len * dir_part
    meta_gradient = lax.psum(new_solution, "task") / lax.axis_size("task")
    return (new_solution[None], new_residual[None], new_direction[None], meta_gradient)


def solution(mesh):
    in_specs = (
        P("task", "ctx", None),
        P("task", "ctx", None),
        P("task", None, None),
        P("task", "ctx", None),
        P("task", "ctx", None),
        P("task", "ctx", None),
        P("task", "ctx"),
        P("task", None),
        P("task", None),
        P("task", None),
        P("task"),
    )
    out_specs = (P("task", "ctx"), P("task", "ctx"), P("task", "ctx"), P("ctx"))
    return jax.shard_map(
        per_device, mesh=mesh, in_specs=in_specs, out_specs=out_specs, check_vma=False
    )
```

profile of v0, /device:TPU:8, one launch (start us, length us, event | category | flops | bytes accessed | tf_op | source)
XLA Modules:
  0.0 247.7 jit_solution(12830081265267951997)
XLA Ops:
  7.2 4.6 %collective-permute-start = (s32[128]{0:T(128)}, s32[128]{0:T(128)S(1)}, u32[]{:S(2)}, u32[]{:S(2)}) collective-permute-start(s32[128]{0:T(128)} %bitcast.348), channel_id=1, source_target_pairs={{0,6},{1,7},{2,8},{3,9},{4,10},{5,11},{6,12},{7,13},{8,14},{9,15},... | collective-permute-start | bytes 1544 | tf_op jit(solution)/shard_map/ppermute | solution.py:16
  11.8 2.6 %collective-permute-start.1 = (s32[128]{0:T(128)}, s32[128]{0:T(128)S(1)}, u32[]{:S(2)}, u32[]{:S(2)}) collective-permute-start(s32[128]{0:T(128)} %bitcast.349), channel_id=1, source_target_pairs={{0,5},{1,6},{2,7},{3,8},{4,9},{5,10},{6,11},{7,12},{8,13},{9,14},{... | collective-permute-start | bytes 1544 | tf_op jit(solution)/shard_map/ppermute | solution.py:16
  14.5 2.8 %collective-permute-start.2 = (s32[128]{0:T(128)}, s32[128]{0:T(128)S(1)}, u32[]{:S(2)}, u32[]{:S(2)}) collective-permute-start(s32[128]{0:T(128)} %bitcast.350), channel_id=1, source_target_pairs={{0,4},{1,5},{2,6},{3,7},{4,8},{5,9},{6,10},{7,11},{8,12},{9,13},{1... | collective-permute-start | bytes 1544 | tf_op jit(solution)/shard_map/ppermute | solution.py:16
  17.2 1.9 collective-permute-start.3
  19.2 2.5 %collective-permute-start.4 = (s32[128]{0:T(128)}, s32[128]{0:T(128)S(1)}, u32[]{:S(2)}, u32[]{:S(2)}) collective-permute-start(s32[128]{0:T(128)} %bitcast.352), channel_id=1, source_target_pairs={{0,2},{1,3},{2,4},{3,5},{4,6},{5,7},{6,8},{7,9},{8,10},{9,11},{10,... | collective-permute-start | bytes 1544 | tf_op jit(solution)/shard_map/ppermute | solution.py:16
  32.5 2.5 %collective-permute-start.8 = (bf16[128,512]{1,0:T(8,128)(2,1)S(1)}, bf16[128,512]{1,0:T(8,128)(2,1)S(1)}, u32[]{:S(2)}, u32[]{:S(2)}) collective-permute-start(bf16[128,512]{1,0:T(8,128)(2,1)S(1)} %bitcast.334), channel_id=1, source_target_pairs={{0,4},{1,5},{2,6},{3,7},{4,8},{5,9},{6,10},{7,11},{8,12},{9,13},{1... | collective-permute-start | bytes 393224 | tf_op jit(solution)/shard_map/ppermute | solution.py:16
  35.0 3.1 %collective-permute-start.9 = (bf16[128,512]{1,0:T(8,128)(2,1)S(1)}, bf16[128,512]{1,0:T(8,128)(2,1)S(1)}, u32[]{:S(2)}, u32[]{:S(2)}) collective-permute-start(bf16[128,512]{1,0:T(8,128)(2,1)S(1)} %bitcast.335), channel_id=1, source_target_pairs={{0,3},{1,4},{2,5},{3,6},{4,7},{5,8},{6,9},{7,10},{8,11},{9,12},{10... | collective-permute-start | bytes 393224 | tf_op jit(solution)/shard_map/ppermute | solution.py:16
  38.2 2.2 collective-permute-start.10
  40.6 2.1 collective-permute-start.11
  45.4 3.8 %collective-permute-start.14 = (bf16[128,512]{1,0:T(8,128)(2,1)S(1)}, bf16[128,512]{1,0:T(8,128)(2,1)S(1)}, u32[]{:S(2)}, u32[]{:S(2)}) collective-permute-start(bf16[128,512]{1,0:T(8,128)(2,1)S(1)} %bitcast.340), channel_id=1, source_target_pairs={{0,4},{1,5},{2,6},{3,7},{4,8},{5,9},{6,10},{7,11},{8,12},{9,13},{1... | collective-permute-start | bytes 393224 | tf_op jit(solution)/shard_map/ppermute | solution.py:16
  49.2 4.9 %collective-permute-start.15 = (bf16[128,512]{1,0:T(8,128)(2,1)S(1)}, bf16[128,512]{1,0:T(8,128)(2,1)S(1)}, u32[]{:S(2)}, u32[]{:S(2)}) collective-permute-start(bf16[128,512]{1,0:T(8,128)(2,1)S(1)} %bitcast.341), channel_id=1, source_target_pairs={{0,3},{1,4},{2,5},{3,6},{4,7},{5,8},{6,9},{7,10},{8,11},{9,12},{10... | collective-permute-start | bytes 393224 | tf_op jit(solution)/shard_map/ppermute | solution.py:16
  54.1 5.8 %collective-permute-start.16 = (bf16[128,512]{1,0:T(8,128)(2,1)S(1)}, bf16[128,512]{1,0:T(8,128)(2,1)S(1)}, u32[]{:S(2)}, u32[]{:S(2)}) collective-permute-start(bf16[128,512]{1,0:T(8,128)(2,1)S(1)} %bitcast.342), channel_id=1, source_target_pairs={{0,2},{1,3},{2,4},{3,5},{4,6},{5,7},{6,8},{7,9},{8,10},{9,11},{10,... | collective-permute-start | bytes 393224 | tf_op jit(solution)/shard_map/ppermute | solution.py:16
  60.0 4.2 %collective-permute-start.17 = (bf16[128,512]{1,0:T(8,128)(2,1)S(1)}, bf16[128,512]{1,0:T(8,128)(2,1)S(1)}, u32[]{:S(2)}, u32[]{:S(2)}) collective-permute-start(bf16[128,512]{1,0:T(8,128)(2,1)S(1)} %bitcast.343), channel_id=1, source_target_pairs={{0,1},{1,2},{2,3},{3,4},{4,5},{5,6},{6,7},{7,8},{8,9},{9,10},{10,1... | collective-permute-start | bytes 393224 | tf_op jit(solution)/shard_map/ppermute | solution.py:16
  64.3 4.6 %collective-permute-done.17 = bf16[128,512]{1,0:T(8,128)(2,1)S(1)} collective-permute-done((bf16[128,512]{1,0:T(8,128)(2,1)S(1)}, bf16[128,512]{1,0:T(8,128)(2,1)S(1)}, u32[]{:S(2)}, u32[]{:S(2)}) %collective-permute-start.17) | collective-permute-done | bytes 131104 | tf_op jit(solution)/shard_map/ppermute | solution.py:16
  69.0 3.1 %fusion.228 = (f32[128,4]{0,1:T(4,128)S(1)}, f32[128,4,896]{2,0,1:T(8,128)}) fusion(pred[128,896]{1,0:T(8,128)(4,1)S(1)} %compare_and_fusion, bf16[16,4,8,128]{3,2,1,0:T(8,128)(2,1)S(1)} %copy-done.11, bf16[896,512]{1,0:T(8,128)(2,1)} %copy-done.15), kind=kOutput, calls=%fused_computation.226 | convolution fusion | flops 119276416 | bytes 2312192 | tf_op jit(solution)/shard_map/sub | solution.py:44
  72.1 2.1 fusion.221
  77.6 2.1 fusion.214
  81.4 2.1 fusion.207
  83.9 3.4 %fusion.9 = f32[128,4,896]{2,0,1:T(8,128)} fusion(bf16[128,4,128]{0,2,1:T(8,128)(2,1)S(1)} %bitcast.331, bf16[896,512]{1,0:T(8,128)(2,1)S(1)} %constant_dynamic-update-slice_fusion.8, f32[128,4,896]{2,0,1:T(8,128)} %get-tuple-element.35, f32[128,4]{0,1:T(4,128)S(1)} %get-tuple-element.34), kind=kOutput, calls=%fused_computation.9 | convolution fusion | flops 118359424 | bytes 4032512 | tf_op jit(solution)/shard_map/sub | solution.py:48
  87.3 5.7 %multiply_reduce_fusion.6 = (f32[128,4]{0,1:T(4,128)S(1)}, f32[128,4,896]{2,0,1:T(8,128)}) fusion(f32[128,4,896]{2,0,1:T(8,128)} %get-tuple-element.35, f32[128,4]{0,1:T(4,128)S(1)} %get-tuple-element.34, f32[128,4,896]{2,0,1:T(8,128)} %fusion.9, f32[896,128,4]{0,1,2:T(8,128)} %fusion.75, bf16[16,4,8,128]{3,2,1,0:T(8,128)(2,1)} %get-tuple-element.8, ...), kind=kOutput, calls=%fused_computation.46 | convolution fusion | flops 239469440 | bytes 9902080 | tf_op jit(solution)/shard_map/sub | solution.py:48
  93.0 3.8 %fusion.37 = bf16[128,4,128]{0,2,1:T(8,128)(2,1)} fusion(f32[128,4,896]{2,0,1:T(8,128)} %get-tuple-element.37, f32[128,4]{0,1:T(4,128)S(1)} %get-tuple-element.36, bf16[896,512]{1,0:T(8,128)(2,1)} %copy-done.15, f32[128,4]{0,1:T(4,128)S(1)} %get-tuple-element.34, pred[128,896]{1,0:T(8,128)(4,1)} %copy-done.13, bf16[16,4,8,128]{3,2,1,0:T(8,128)(2,1)} %get-tuple-element.12), kind=kOutput, calls=%fused_computation.63 | convolution fusion | flops 238224768 | bytes 2674688 | tf_op jit(solution)/shard_map/tgk,kd->tgd/dot_general | solution.py:52
  96.8 3.4 %fusion.6 = f32[128,4,896]{2,0,1:T(8,128)} fusion(bf16[128,4,128]{0,2,1:T(8,128)(2,1)S(1)} %bitcast.329, bf16[896,512]{1,0:T(8,128)(2,1)S(1)} %constant_dynamic-update-slice_fusion.8, f32[128,4,896]{2,0,1:T(8,128)} %get-tuple-element.31, f32[128,4]{0,1:T(4,128)S(1)} %get-tuple-element.30), kind=kOutput, calls=%fused_computation.6 | convolution fusion | flops 118359424 | bytes 4032512 | tf_op jit(solution)/shard_map/sub | solution.py:48
  100.2 5.6 %multiply_reduce_fusion.4 = (f32[128,4]{0,1:T(4,128)S(1)}, f32[128,4,896]{2,0,1:T(8,128)}) fusion(f32[128,4,896]{2,0,1:T(8,128)} %get-tuple-element.31, f32[128,4]{0,1:T(4,128)S(1)} %get-tuple-element.30, f32[128,4,896]{2,0,1:T(8,128)} %fusion.6, f32[896,128,4]{0,1,2:T(8,128)} %fusion.74, bf16[16,4,8,128]{3,2,1,0:T(8,128)(2,1)S(1)} %copy-done.12, ...), kind=kOutput, calls=%fused_computation.40 | convolution fusion | flops 239469440 | bytes 9902080 | tf_op jit(solution)/shard_map/sub | solution.py:48
  105.8 3.2 %fusion.38 = bf16[128,4,128]{0,2,1:T(8,128)(2,1)S(1)} fusion(f32[128,4,896]{2,0,1:T(8,128)} %get-tuple-element.33, f32[128,4]{0,1:T(4,128)S(1)} %get-tuple-element.32, bf16[896,512]{1,0:T(8,128)(2,1)} %copy-done.15, f32[128,4]{0,1:T(4,128)S(1)} %get-tuple-element.30, pred[128,896]{1,0:T(8,128)(4,1)} %copy-done.13, bf16[16,4,8,128]{3,2,1,0:T(8,128)(2,1)} %copy-done.9), kind=kOutput, calls=%fused_computation.64 | convolution fusion | flops 238224768 | bytes 2674688 | tf_op jit(solution)/shard_map/tgk,kd->tgd/dot_general | solution.py:52
  109.0 3.4 %fusion.3 = f32[128,4,896]{2,0,1:T(8,128)} fusion(bf16[128,4,128]{0,2,1:T(8,128)(2,1)S(1)} %bitcast.327, bf16[896,512]{1,0:T(8,128)(2,1)S(1)} %constant_dynamic-update-slice_fusion.8, f32[128,4,896]{2,0,1:T(8,128)} %get-tuple-element.27, f32[128,4]{0,1:T(4,128)S(1)} %get-tuple-element.26), kind=kOutput, calls=%fused_computation.3 | convolution fusion | flops 118359424 | bytes 4032512 | tf_op jit(solution)/shard_map/sub | solution.py:48
  112.4 5.8 %multiply_reduce_fusion.2 = (f32[128,4]{0,1:T(4,128)S(1)}, f32[128,4,896]{2,0,1:T(8,128)}) fusion(f32[128,4,896]{2,0,1:T(8,128)} %get-tuple-element.27, f32[128,4]{0,1:T(4,128)S(1)} %get-tuple-element.26, f32[128,4,896]{2,0,1:T(8,128)} %fusion.3, f32[896,128,4]{0,1,2:T(8,128)} %fusion.73, bf16[16,4,8,128]{3,2,1,0:T(8,128)(2,1)S(1)} %copy-done.10, ...), kind=kOutput, calls=%fused_computation.34 | convolution fusion | flops 239469440 | bytes 9902080 | tf_op jit(solution)/shard_map/sub | solution.py:48
  118.2 3.2 %fusion.39 = bf16[128,4,128]{0,2,1:T(8,128)(2,1)S(1)} fusion(f32[128,4,896]{2,0,1:T(8,128)} %get-tuple-element.29, f32[128,4]{0,1:T(4,128)S(1)} %get-tuple-element.28, bf16[896,512]{1,0:T(8,128)(2,1)} %copy-done.15, f32[128,4]{0,1:T(4,128)S(1)} %get-tuple-element.26, pred[128,896]{1,0:T(8,128)(4,1)} %copy-done.13, bf16[16,4,8,128]{3,2,1,0:T(8,128)(2,1)} %copy-done.7), kind=kOutput, calls=%fused_computation.65 | convolution fusion | flops 238224768 | bytes 2674688 | tf_op jit(solution)/shard_map/tgk,kd->tgd/dot_general | solution.py:52
  121.4 3.3 %fusion = f32[128,4,896]{2,0,1:T(8,128)} fusion(bf16[128,4,128]{0,2,1:T(8,128)(2,1)S(1)} %bitcast.325, bf16[896,512]{1,0:T(8,128)(2,1)S(1)} %constant_dynamic-update-slice_fusion.8, f32[128,4,896]{2,0,1:T(8,128)} %get-tuple-element.23, f32[128,4]{0,1:T(4,128)S(1)} %get-tuple-element.22), kind=kOutput, calls=%fused_computation | convolution fusion | flops 118359424 | bytes 4032512 | tf_op jit(solution)/shard_map/sub | solution.py:48
  124.8 5.1 %multiply_reduce_fusion = (f32[128,4]{0,1:T(4,128)S(1)}, f32[128,4,896]{2,0,1:T(8,128)}) fusion(f32[128,4,896]{2,0,1:T(8,128)} %get-tuple-element.23, f32[128,4]{0,1:T(4,128)S(1)} %get-tuple-element.22, f32[128,4,896]{2,0,1:T(8,128)} %fusion, f32[896,128,4]{0,1,2:T(8,128)S(1)} %fusion.72, bf16[16,4,8,128]{3,2,1,0:T(8,128)(2,1)S(1)} %copy-done.8, ...), kind=kOutput, calls=%fused_computation.28 | convolution fusion | flops 239469440 | bytes 9902080 | tf_op jit(solution)/shard_map/sub | solution.py:48
  129.9 3.2 %fusion.40 = bf16[128,4,128]{0,2,1:T(8,128)(2,1)S(1)} fusion(f32[128,4,896]{2,0,1:T(8,128)} %get-tuple-element.25, f32[128,4]{0,1:T(4,128)S(1)} %get-tuple-element.24, bf16[896,512]{1,0:T(8,128)(2,1)S(1)} %copy-done.17, f32[128,4]{0,1:T(4,128)S(1)} %get-tuple-element.22, pred[128,896]{1,0:T(8,128)(4,1)} %copy-done.13, bf16[16,4,8,128]{3,2,1,0:T(8,128)(2,1)} %copy-done.6), kind=kOutput, calls=%fused_computation.66 | convolution fusion | flops 238224768 | bytes 2674688 | tf_op jit(solution)/shard_map/tgk,kd->tgd/dot_general | solution.py:52
  134.6 93.5 %all-reduce.2.cloned.1.call-done = f32[32768]{0:T(1024)} async-done(((f32[32768]{0:T(1024)}), f32[32768]{0:T(1024)}) %all-reduce.2.cloned.1.call-update) | async-done | bytes 131088 | tf_op jit(solution)/shard_map/psum | solution.py:113
  234.6 5.0 %psum.15 = f32[2048]{0:T(1024)S(1)} all-reduce(f32[2048]{0:T(1024)S(1)} %bitcast.344), channel_id=1, replica_groups=mesh['task'=2,'ctx'=16] {'task'}, use_global_device_ids=true, to_apply=%region_24.25 | all-reduce | flops 2048 | bytes 16384 | tf_op jit(solution)/shard_map/psum | solution.py:121
  (113 shorter events, 25.2 us)
Async XLA Ops:
  7.2 14.6 %copy-start = (bf16[1,16,2048]{2,1,0:T(8,128)(2,1)S(1)}, bf16[1,16,2048]{2,1,0:T(8,128)(2,1)}, u32[]{:S(2)}) copy-start(bf16[1,16,2048]{2,1,0:T(8,128)(2,1)} %param.13) | copy-start | bytes 196612
  7.2 16.7 %copy-start.3 = (bf16[1,128,2048]{2,1,0:T(8,128)(2,1)S(1)}, bf16[1,128,2048]{2,1,0:T(8,128)(2,1)}, u32[]{:S(2)}) copy-start(bf16[1,128,2048]{2,1,0:T(8,128)(2,1)} %param.16) | copy-start | bytes 1572868
  7.2 220.9 %all-reduce.2.cloned.1.call-start = ((), (), s32[]{:S(2)}) async-start(), calls=%async_computation | async-start | bytes 262144 | tf_op jit(solution)/shard_map/psum | solution.py:113
  7.2 20.6 %collective-permute-start = (s32[128]{0:T(128)}, s32[128]{0:T(128)S(1)}, u32[]{:S(2)}, u32[]{:S(2)}) collective-permute-start(s32[128]{0:T(128)} %bitcast.348), channel_id=1, source_target_pairs={{0,6},{1,7},{2,8},{3,9},{4,10},{5,11},{6,12},{7,13},{8,14},{9,15},... | collective-permute-start | bytes 1544 | tf_op jit(solution)/shard_map/ppermute | solution.py:16
  11.8 18.0 %collective-permute-start.1 = (s32[128]{0:T(128)}, s32[128]{0:T(128)S(1)}, u32[]{:S(2)}, u32[]{:S(2)}) collective-permute-start(s32[128]{0:T(128)} %bitcast.349), channel_id=1, source_target_pairs={{0,5},{1,6},{2,7},{3,8},{4,9},{5,10},{6,11},{7,12},{8,13},{9,14},{... | collective-permute-start | bytes 1544 | tf_op jit(solution)/shard_map/ppermute | solution.py:16
  14.5 16.7 %collective-permute-start.2 = (s32[128]{0:T(128)}, s32[128]{0:T(128)S(1)}, u32[]{:S(2)}, u32[]{:S(2)}) collective-permute-start(s32[128]{0:T(128)} %bitcast.350), channel_id=1, source_target_pairs={{0,4},{1,5},{2,6},{3,7},{4,8},{5,9},{6,10},{7,11},{8,12},{9,13},{1... | collective-permute-start | bytes 1544 | tf_op jit(solution)/shard_map/ppermute | solution.py:16
  17.2 15.2 %collective-permute-start.3 = (s32[128]{0:T(128)}, s32[128]{0:T(128)S(1)}, u32[]{:S(2)}, u32[]{:S(2)}) collective-permute-start(s32[128]{0:T(128)} %bitcast.351), channel_id=1, source_target_pairs={{0,3},{1,4},{2,5},{3,6},{4,7},{5,8},{6,9},{7,10},{8,11},{9,12},{10... | collective-permute-start | bytes 1544 | tf_op jit(solution)/shard_map/ppermute | solution.py:16
  19.2 15.9 %collective-permute-start.4 = (s32[128]{0:T(128)}, s32[128]{0:T(128)S(1)}, u32[]{:S(2)}, u32[]{:S(2)}) collective-permute-start(s32[128]{0:T(128)} %bitcast.352), channel_id=1, source_target_pairs={{0,2},{1,3},{2,4},{3,5},{4,6},{5,7},{6,8},{7,9},{8,10},{9,11},{10,... | collective-permute-start | bytes 1544 | tf_op jit(solution)/shard_map/ppermute | solution.py:16
  23.9 48.2 %copy-start.9 = (bf16[16,4,8,128]{3,2,1,0:T(8,128)(2,1)}, bf16[16,4,8,128]{3,2,1,0:T(8,128)(2,1)S(1)}, u32[]{:S(2)}) copy-start(bf16[16,4,8,128]{3,2,1,0:T(8,128)(2,1)S(1)} %get-tuple-element.15) | copy-start | bytes 393220
  23.9 53.8 %copy-start.7 = (bf16[16,4,8,128]{3,2,1,0:T(8,128)(2,1)}, bf16[16,4,8,128]{3,2,1,0:T(8,128)(2,1)S(1)}, u32[]{:S(2)}) copy-start(bf16[16,4,8,128]{3,2,1,0:T(8,128)(2,1)S(1)} %get-tuple-element.14) | copy-start | bytes 393220
  23.9 57.5 %copy-start.6 = (bf16[16,4,8,128]{3,2,1,0:T(8,128)(2,1)}, bf16[16,4,8,128]{3,2,1,0:T(8,128)(2,1)S(1)}, u32[]{:S(2)}) copy-start(bf16[16,4,8,128]{3,2,1,0:T(8,128)(2,1)S(1)} %get-tuple-element.13) | copy-start | bytes 393220
  24.1 3.7 %copy-start.19 = (s32[1,128]{1,0:T(1,128)S(1)}, s32[1,128]{1,0:T(1,128)}, u32[]{:S(2)}) copy-start(s32[1,128]{1,0:T(1,128)} %param.17) | copy-start | bytes 1540
  24.2 5.6 %copy-start.4 = (bf16[1,128,512]{2,1,0:T(8,128)(2,1)S(1)}, bf16[1,128,512]{2,1,0:T(8,128)(2,1)}, u32[]{:S(2)}) copy-start(bf16[1,128,512]{2,1,0:T(8,128)(2,1)} %param.14) | copy-start | bytes 393220
  24.2 18.6 %copy-start.5 = (bf16[1,128,512]{2,1,0:T(8,128)(2,1)S(1)}, bf16[1,128,512]{2,1,0:T(8,128)(2,1)}, u32[]{:S(2)}) copy-start(bf16[1,128,512]{2,1,0:T(8,128)(2,1)} %param.15) | copy-start | bytes 393220
  27.8 10.3 %collective-permute-start.5 = (s32[128]{0:T(128)S(1)}, s32[128]{0:T(128)S(1)}, u32[]{:S(2)}, u32[]{:S(2)}) collective-permute-start(s32[128]{0:T(128)S(1)} %bitcast.353), channel_id=1, source_target_pairs={{0,1},{1,2},{2,3},{3,4},{4,5},{5,6},{6,7},{7,8},{8,9},{9,10},{10,1... | collective-permute-start | bytes 1544 | tf_op jit(solution)/shard_map/ppermute | solution.py:16
  29.8 10.8 %collective-permute-start.6 = (bf16[128,512]{1,0:T(8,128)(2,1)S(1)}, bf16[128,512]{1,0:T(8,128)(2,1)S(1)}, u32[]{:S(2)}, u32[]{:S(2)}) collective-permute-start(bf16[128,512]{1,0:T(8,128)(2,1)S(1)} %bitcast.332), channel_id=1, source_target_pairs={{0,6},{1,7},{2,8},{3,9},{4,10},{5,11},{6,12},{7,13},{8,14},{9,15},... | collective-permute-start | bytes 393224 | tf_op jit(solution)/shard_map/ppermute | solution.py:16
  31.1 11.6 %collective-permute-start.7 = (bf16[128,512]{1,0:T(8,128)(2,1)S(1)}, bf16[128,512]{1,0:T(8,128)(2,1)S(1)}, u32[]{:S(2)}, u32[]{:S(2)}) collective-permute-start(bf16[128,512]{1,0:T(8,128)(2,1)S(1)} %bitcast.333), channel_id=1, source_target_pairs={{0,5},{1,6},{2,7},{3,8},{4,9},{5,10},{6,11},{7,12},{8,13},{9,14},{... | collective-permute-start | bytes 393224 | tf_op jit(solution)/shard_map/ppermute | solution.py:16
  32.5 11.6 %collective-permute-start.8 = (bf16[128,512]{1,0:T(8,128)(2,1)S(1)}, bf16[128,512]{1,0:T(8,128)(2,1)S(1)}, u32[]{:S(2)}, u32[]{:S(2)}) collective-permute-start(bf16[128,512]{1,0:T(8,128)(2,1)S(1)} %bitcast.334), channel_id=1, source_target_pairs={{0,4},{1,5},{2,6},{3,7},{4,8},{5,9},{6,10},{7,11},{8,12},{9,13},{1... | collective-permute-start | bytes 393224 | tf_op jit(solution)/shard_map/ppermute | solution.py:16
  35.0 10.4 %collective-permute-start.9 = (bf16[128,512]{1,0:T(8,128)(2,1)S(1)}, bf16[128,512]{1,0:T(8,128)(2,1)S(1)}, u32[]{:S(2)}, u32[]{:S(2)}) collective-permute-start(bf16[128,512]{1,0:T(8,128)(2,1)S(1)} %bitcast.335), channel_id=1, source_target_pairs={{0,3},{1,4},{2,5},{3,6},{4,7},{5,8},{6,9},{7,10},{8,11},{9,12},{10... | collective-permute-start | bytes 393224 | tf_op jit(solution)/shard_map/ppermute | solution.py:16
  38.2 11.0 %collective-permute-start.10 = (bf16[128,512]{1,0:T(8,128)(2,1)S(1)}, bf16[128,512]{1,0:T(8,128)(2,1)S(1)}, u32[]{:S(2)}, u32[]{:S(2)}) collective-permute-start(bf16[128,512]{1,0:T(8,128)(2,1)S(1)} %bitcast.336), channel_id=1, source_target_pairs={{0,2},{1,3},{2,4},{3,5},{4,6},{5,7},{6,8},{7,9},{8,10},{9,11},{10,... | collective-permute-start | bytes 393224 | tf_op jit(solution)/shard_map/ppermute | solution.py:16
  40.6 40.8 %copy-start.13 = (pred[128,896]{1,0:T(8,128)(4,1)}, pred[128,896]{1,0:T(8,128)(4,1)S(1)}, u32[]{:S(2)}) copy-start(pred[128,896]{1,0:T(8,128)(4,1)S(1)} %compare_and_fusion) | copy-start | bytes 344068
  40.6 28.3 %copy-start.11 = (bf16[16,4,8,128]{3,2,1,0:T(8,128)(2,1)S(1)}, bf16[16,4,8,128]{3,2,1,0:T(8,128)(2,1)}, u32[]{:S(2)}) copy-start(bf16[16,4,8,128]{3,2,1,0:T(8,128)(2,1)} %get-tuple-element.12) | copy-start | bytes 393220
  40.6 13.5 %collective-permute-start.11 = (bf16[128,512]{1,0:T(8,128)(2,1)S(1)}, bf16[128,512]{1,0:T(8,128)(2,1)S(1)}, u32[]{:S(2)}, u32[]{:S(2)}) collective-permute-start(bf16[128,512]{1,0:T(8,128)(2,1)S(1)} %bitcast.337), channel_id=1, source_target_pairs={{0,1},{1,2},{2,3},{3,4},{4,5},{5,6},{6,7},{7,8},{8,9},{9,10},{10,1... | collective-permute-start | bytes 393224 | tf_op jit(solution)/shard_map/ppermute | solution.py:16
  42.7 17.3 %collective-permute-start.12 = (bf16[128,512]{1,0:T(8,128)(2,1)S(1)}, bf16[128,512]{1,0:T(8,128)(2,1)S(1)}, u32[]{:S(2)}, u32[]{:S(2)}) collective-permute-start(bf16[128,512]{1,0:T(8,128)(2,1)S(1)} %bitcast.338), channel_id=1, source_target_pairs={{0,6},{1,7},{2,8},{3,9},{4,10},{5,11},{6,12},{7,13},{8,14},{9,15},... | collective-permute-start | bytes 393224 | tf_op jit(solution)/shard_map/ppermute | solution.py:16
  44.1 20.2 %collective-permute-start.13 = (bf16[128,512]{1,0:T(8,128)(2,1)S(1)}, bf16[128,512]{1,0:T(8,128)(2,1)S(1)}, u32[]{:S(2)}, u32[]{:S(2)}) collective-permute-start(bf16[128,512]{1,0:T(8,128)(2,1)S(1)} %bitcast.339), channel_id=1, source_target_pairs={{0,5},{1,6},{2,7},{3,8},{4,9},{5,10},{6,11},{7,12},{8,13},{9,14},{... | collective-permute-start | bytes 393224 | tf_op jit(solution)/shard_map/ppermute | solution.py:16
  45.4 18.9 %collective-permute-start.14 = (bf16[128,512]{1,0:T(8,128)(2,1)S(1)}, bf16[128,512]{1,0:T(8,128)(2,1)S(1)}, u32[]{:S(2)}, u32[]{:S(2)}) collective-permute-start(bf16[128,512]{1,0:T(8,128)(2,1)S(1)} %bitcast.340), channel_id=1, source_target_pairs={{0,4},{1,5},{2,6},{3,7},{4,8},{5,9},{6,10},{7,11},{8,12},{9,13},{1... | collective-permute-start | bytes 393224 | tf_op jit(solution)/shard_map/ppermute | solution.py:16
  49.2 15.1 %collective-permute-start.15 = (bf16[128,512]{1,0:T(8,128)(2,1)S(1)}, bf16[128,512]{1,0:T(8,128)(2,1)S(1)}, u32[]{:S(2)}, u32[]{:S(2)}) collective-permute-start(bf16[128,512]{1,0:T(8,128)(2,1)S(1)} %bitcast.341), channel_id=1, source_target_pairs={{0,3},{1,4},{2,5},{3,6},{4,7},{5,8},{6,9},{7,10},{8,11},{9,12},{10... | collective-permute-start | bytes 393224 | tf_op jit(solution)/shard_map/ppermute | solution.py:16
  54.1 10.2 %collective-permute-start.16 = (bf16[128,512]{1,0:T(8,128)(2,1)S(1)}, bf16[128,512]{1,0:T(8,128)(2,1)S(1)}, u32[]{:S(2)}, u32[]{:S(2)}) collective-permute-start(bf16[128,512]{1,0:T(8,128)(2,1)S(1)} %bitcast.342), channel_id=1, source_target_pairs={{0,2},{1,3},{2,4},{3,5},{4,6},{5,7},{6,8},{7,9},{8,10},{9,11},{10,... | collective-permute-start | bytes 393224 | tf_op jit(solution)/shard_map/ppermute | solution.py:16
  60.0 9.0 %copy-start.15 = (bf16[896,512]{1,0:T(8,128)(2,1)}, bf16[896,512]{1,0:T(8,128)(2,1)S(1)}, u32[]{:S(2)}) copy-start(bf16[896,512]{1,0:T(8,128)(2,1)S(1)} %constant_dynamic-update-slice_fusion.1) | copy-start | bytes 2752516
  60.0 8.9 %collective-permute-start.17 = (bf16[128,512]{1,0:T(8,128)(2,1)S(1)}, bf16[128,512]{1,0:T(8,128)(2,1)S(1)}, u32[]{:S(2)}, u32[]{:S(2)}) collective-permute-start(bf16[128,512]{1,0:T(8,128)(2,1)S(1)} %bitcast.343), channel_id=1, source_target_pairs={{0,1},{1,2},{2,3},{3,4},{4,5},{5,6},{6,7},{7,8},{8,9},{9,10},{10,1... | collective-permute-start | bytes 393224 | tf_op jit(solution)/shard_map/ppermute | solution.py:16
  124.8 5.1 %copy-start.17 = (bf16[896,512]{1,0:T(8,128)(2,1)S(1)}, bf16[896,512]{1,0:T(8,128)(2,1)}, u32[]{:S(2)}) copy-start(bf16[896,512]{1,0:T(8,128)(2,1)} %copy-done.15) | copy-start | bytes 2752516
  234.6 6.2 %copy-start.14 = (f32[1,2048]{1,0:T(1,128)}, f32[1,2048]{1,0:T(1,128)S(1)}, u32[]{:S(2)}) copy-start(f32[1,2048]{1,0:T(1,128)S(1)} %get-tuple-element.21) | copy-start | bytes 24580
  (8 other events, 21.6 us)
Sparse Core Ops, SparseCore 0:
  134.1 93.9 all-reduce.1
where the time goes:
time: 249 us; the launch traced here: 248 us
  waiting for transfers between devices  98.1 us (39%)
  matrix products  66.2 us (27%)
  starting transfers between devices  50.1 us (20%)
  between operations  18.1 us (7%)
  other arithmetic  6.81 us (3%)
  blocking collectives  5 us (2%)
  local copies, waits for them, and re-layouts  3.33 us (1%)
    psum x1, waiting for transfers between devices, per_device(): complete_curvature_product = lax.psum(curvature_product_term, 'ctx')  93.5 us
    ppermute x18, starting transfers between devices, passed_along(): lax.ppermute(value, axis, [(source, source + steps) for source in range(l...  50.1 us
    sub x8, matrix products, attend(): centred = (slopes - mean_slope) * (pulls - mean_pull)  35.7 us
    dot_general x4, matrix products, attend(): jnp.einsum('tgk,kd->tgd', coef_rounded, key_head, preferred_element_type=...  13.3 us
    sub x4, matrix products, attend(): exp_terms = jnp.exp(masked - row_max)  9.36 us
    dot_general x4, matrix products, attend(): jnp.einsum('tgd,kd->tgk', grad_head, value_head, preferred_element_type=j...  5.59 us
    psum x1, blocking collectives, per_device(): meta_gradient = lax.psum(new_solution, 'task') / lax.axis_size('task')  5 us
  transfers between devices with their start and end apart: 19, of which 2 were waited for; matrix products, arithmetic and copies ran while one was open for 3% of the time, Pallas kernels for 0%

commit v1 on v0

--- a/solution.py
+++ b/solution.py
@@ -110,7 +110,7 @@
     part_start = dev_index * part_size
     dir_part = lax.dynamic_slice_in_dim(dir_full, part_start, part_size, 0)
     sol_part = lax.dynamic_slice_in_dim(solution[0], part_start, part_size, 0)
-    complete_curvature_product = lax.psum(curvature_product_term, "ctx")
+    complete_curvature_product = jnp.sum(lax.all_gather(curvature_product_term, "ctx"), axis=0)
     curved = dir_full + complete_curvature_product / damp_val
     step_len = old_norm / jnp.sum(dir_full * curved)
     res_next = res_full - step_len * curved

time: 249 us -> 202 us (0.81); the launches traced: 248 us -> 198 us
  waiting for transfers between devices: 98.1 us -> 46.9 us
    psum x1 -> x0, waiting for transfers between devices: 93.5 us -> none  [per_device(): complete_curvature_product = lax.psum(curvature_product_term, 'ctx')]
    all_gather x0 -> x1, waiting for transfers between devices: none -> 42.3 us  [per_device(): lax.all_gather(curvature_product_term, 'ctx')]
    reduce_sum x0 -> x1, other arithmetic: none -> 2.95 us  [per_device(): jnp.sum(lax.all_gather(curvature_product_term, 'ctx'), axis=0)]
where the time goes in v1:
time: 202 us; the launch traced here: 198 us
  matrix products  66.2 us (33%)
  starting transfers between devices  50.1 us (25%)
  waiting for transfers between devices  46.9 us (23%)
  between operations  18.1 us (9%)
  other arithmetic  7.95 us (4%)
  blocking collectives  5 us (2%)
  local copies, waits for them, and re-layouts  3.46 us (2%)
    ppermute x18, starting transfers between devices, passed_along(): lax.ppermute(value, axis, [(source, source + steps) for source in range(l...  50.1 us
    all_gather x1, waiting for transfers between devices, per_device(): lax.all_gather(curvature_product_term, 'ctx')  42.3 us
    sub x8, matrix products, attend(): centred = (slopes - mean_slope) * (pulls - mean_pull)  35.7 us
    dot_general x4, matrix products, attend(): jnp.einsum('tgk,kd->tgd', coef_rounded, key_head, preferred_element_type=...  13.3 us
    sub x4, matrix products, attend(): exp_terms = jnp.exp(masked - row_max)  9.36 us
    dot_general x4, matrix products, attend(): jnp.einsum('tgd,kd->tgk', grad_head, value_head, preferred_element_type=j...  5.6 us
    psum x1, blocking collectives, per_device(): meta_gradient = lax.psum(new_solution, 'task') / lax.axis_size('task')  5 us
    ppermute x18, waiting for transfers between devices, passed_along(): lax.ppermute(value, axis, [(source, source + steps) for source in range(l...  4.6 us
  transfers between devices with their start and end apart: 19, of which 2 were waited for; matrix products, arithmetic and copies ran while one was open for 3% of the time, Pallas kernels for 0%

profile of v1, /device:TPU:8, one launch (start us, length us, event | category | flops | bytes accessed | tf_op | source)
XLA Modules:
  0.0 197.8 jit_solution(4780390406674372984)
XLA Ops:
  7.2 4.6 %collective-permute-start = (s32[128]{0:T(128)}, s32[128]{0:T(128)S(1)}, u32[]{:S(2)}, u32[]{:S(2)}) collective-permute-start(s32[128]{0:T(128)} %bitcast.345), channel_id=1, source_target_pairs={{0,6},{1,7},{2,8},{3,9},{4,10},{5,11},{6,12},{7,13},{8,14},{9,15},... | collective-permute-start | bytes 1544 | tf_op jit(solution)/shard_map/ppermute | solution.py:16
  11.8 2.6 %collective-permute-start.1 = (s32[128]{0:T(128)}, s32[128]{0:T(128)S(1)}, u32[]{:S(2)}, u32[]{:S(2)}) collective-permute-start(s32[128]{0:T(128)} %bitcast.346), channel_id=1, source_target_pairs={{0,5},{1,6},{2,7},{3,8},{4,9},{5,10},{6,11},{7,12},{8,13},{9,14},{... | collective-permute-start | bytes 1544 | tf_op jit(solution)/shard_map/ppermute | solution.py:16
  14.5 2.8 %collective-permute-start.2 = (s32[128]{0:T(128)}, s32[128]{0:T(128)S(1)}, u32[]{:S(2)}, u32[]{:S(2)}) collective-permute-start(s32[128]{0:T(128)} %bitcast.347), channel_id=1, source_target_pairs={{0,4},{1,5},{2,6},{3,7},{4,8},{5,9},{6,10},{7,11},{8,12},{9,13},{1... | collective-permute-start | bytes 1544 | tf_op jit(solution)/shard_map/ppermute | solution.py:16
  19.2 2.5 %collective-permute-start.4 = (s32[128]{0:T(128)}, s32[128]{0:T(128)S(1)}, u32[]{:S(2)}, u32[]{:S(2)}) collective-permute-start(s32[128]{0:T(128)} %bitcast.349), channel_id=1, source_target_pairs={{0,2},{1,3},{2,4},{3,5},{4,6},{5,7},{6,8},{7,9},{8,10},{9,11},{10,... | collective-permute-start | bytes 1544 | tf_op jit(solution)/shard_map/ppermute | solution.py:16
  31.8 2.6 %collective-permute-start.8 = (bf16[128,512]{1,0:T(8,128)(2,1)S(1)}, bf16[128,512]{1,0:T(8,128)(2,1)S(1)}, u32[]{:S(2)}, u32[]{:S(2)}) collective-permute-start(bf16[128,512]{1,0:T(8,128)(2,1)S(1)} %bitcast.331), channel_id=1, source_target_pairs={{0,4},{1,5},{2,6},{3,7},{4,8},{5,9},{6,10},{7,11},{8,12},{9,13},{1... | collective-permute-start | bytes 393224 | tf_op jit(solution)/shard_map/ppermute | solution.py:16
  34.4 3.1 %collective-permute-start.9 = (bf16[128,512]{1,0:T(8,128)(2,1)S(1)}, bf16[128,512]{1,0:T(8,128)(2,1)S(1)}, u32[]{:S(2)}, u32[]{:S(2)}) collective-permute-start(bf16[128,512]{1,0:T(8,128)(2,1)S(1)} %bitcast.332), channel_id=1, source_target_pairs={{0,3},{1,4},{2,5},{3,6},{4,7},{5,8},{6,9},{7,10},{8,11},{9,12},{10... | collective-permute-start | bytes 393224 | tf_op jit(solution)/shard_map/ppermute | solution.py:16
  37.5 2.2 %collective-permute-start.10 = (bf16[128,512]{1,0:T(8,128)(2,1)S(1)}, bf16[128,512]{1,0:T(8,128)(2,1)S(1)}, u32[]{:S(2)}, u32[]{:S(2)}) collective-permute-start(bf16[128,512]{1,0:T(8,128)(2,1)S(1)} %bitcast.333), channel_id=1, source_target_pairs={{0,2},{1,3},{2,4},{3,5},{4,6},{5,7},{6,8},{7,9},{8,10},{9,11},{10,... | collective-permute-start | bytes 393224 | tf_op jit(solution)/shard_map/ppermute | solution.py:16
  40.0 2.1 %collective-permute-start.11 = (bf16[128,512]{1,0:T(8,128)(2,1)S(1)}, bf16[128,512]{1,0:T(8,128)(2,1)S(1)}, u32[]{:S(2)}, u32[]{:S(2)}) collective-permute-start(bf16[128,512]{1,0:T(8,128)(2,1)S(1)} %bitcast.334), channel_id=1, source_target_pairs={{0,1},{1,2},{2,3},{3,4},{4,5},{5,6},{6,7},{7,8},{8,9},{9,10},{10,1... | collective-permute-start | bytes 393224 | tf_op jit(solution)/shard_map/ppermute | solution.py:16
  44.7 3.9 %collective-permute-start.14 = (bf16[128,512]{1,0:T(8,128)(2,1)S(1)}, bf16[128,512]{1,0:T(8,128)(2,1)S(1)}, u32[]{:S(2)}, u32[]{:S(2)}) collective-permute-start(bf16[128,512]{1,0:T(8,128)(2,1)S(1)} %bitcast.337), channel_id=1, source_target_pairs={{0,4},{1,5},{2,6},{3,7},{4,8},{5,9},{6,10},{7,11},{8,12},{9,13},{1... | collective-permute-start | bytes 393224 | tf_op jit(solution)/shard_map/ppermute | solution.py:16
  48.6 4.9 %collective-permute-start.15 = (bf16[128,512]{1,0:T(8,128)(2,1)S(1)}, bf16[128,512]{1,0:T(8,128)(2,1)S(1)}, u32[]{:S(2)}, u32[]{:S(2)}) collective-permute-start(bf16[128,512]{1,0:T(8,128)(2,1)S(1)} %bitcast.338), channel_id=1, source_target_pairs={{0,3},{1,4},{2,5},{3,6},{4,7},{5,8},{6,9},{7,10},{8,11},{9,12},{10... | collective-permute-start | bytes 393224 | tf_op jit(solution)/shard_map/ppermute | solution.py:16
  53.6 5.8 %collective-permute-start.16 = (bf16[128,512]{1,0:T(8,128)(2,1)S(1)}, bf16[128,512]{1,0:T(8,128)(2,1)S(1)}, u32[]{:S(2)}, u32[]{:S(2)}) collective-permute-start(bf16[128,512]{1,0:T(8,128)(2,1)S(1)} %bitcast.339), channel_id=1, source_target_pairs={{0,2},{1,3},{2,4},{3,5},{4,6},{5,7},{6,8},{7,9},{8,10},{9,11},{10,... | collective-permute-start | bytes 393224 | tf_op jit(solution)/shard_map/ppermute | solution.py:16
  59.4 4.1 %collective-permute-start.17 = (bf16[128,512]{1,0:T(8,128)(2,1)S(1)}, bf16[128,512]{1,0:T(8,128)(2,1)S(1)}, u32[]{:S(2)}, u32[]{:S(2)}) collective-permute-start(bf16[128,512]{1,0:T(8,128)(2,1)S(1)} %bitcast.340), channel_id=1, source_target_pairs={{0,1},{1,2},{2,3},{3,4},{4,5},{5,6},{6,7},{7,8},{8,9},{9,10},{10,1... | collective-permute-start | bytes 393224 | tf_op jit(solution)/shard_map/ppermute | solution.py:16
  63.7 4.6 %collective-permute-done.17 = bf16[128,512]{1,0:T(8,128)(2,1)S(1)} collective-permute-done((bf16[128,512]{1,0:T(8,128)(2,1)S(1)}, bf16[128,512]{1,0:T(8,128)(2,1)S(1)}, u32[]{:S(2)}, u32[]{:S(2)}) %collective-permute-start.17) | collective-permute-done | bytes 131104 | tf_op jit(solution)/shard_map/ppermute | solution.py:16
  68.3 3.1 %fusion.228 = (f32[128,4]{0,1:T(4,128)S(1)}, f32[128,4,896]{2,0,1:T(8,128)}) fusion(pred[128,896]{1,0:T(8,128)(4,1)S(1)} %compare_and_fusion, bf16[16,4,8,128]{3,2,1,0:T(8,128)(2,1)S(1)} %copy-done.11, bf16[896,512]{1,0:T(8,128)(2,1)} %copy-done.15), kind=kOutput, calls=%fused_computation.226 | convolution fusion | flops 119276416 | bytes 2312192 | tf_op jit(solution)/shard_map/sub | solution.py:44
  71.4 2.1 %fusion.221 = (f32[128,4]{0,1:T(4,128)S(1)}, f32[128,4,896]{2,0,1:T(8,128)}) fusion(pred[128,896]{1,0:T(8,128)(4,1)S(1)} %compare_and_fusion, bf16[16,4,8,128]{3,2,1,0:T(8,128)(2,1)S(1)} %get-tuple-element.15, bf16[896,512]{1,0:T(8,128)(2,1)S(1)} %copy-done.16), kind=kOutput, calls=%fused_computation.225 | convolution fusion | flops 119276416 | bytes 2312192 | tf_op jit(solution)/shard_map/sub | solution.py:44
  77.0 2.1 %fusion.214 = (f32[128,4]{0,1:T(4,128)S(1)}, f32[128,4,896]{2,0,1:T(8,128)}) fusion(pred[128,896]{1,0:T(8,128)(4,1)S(1)} %compare_and_fusion, bf16[16,4,8,128]{3,2,1,0:T(8,128)(2,1)S(1)} %get-tuple-element.14, bf16[896,512]{1,0:T(8,128)(2,1)S(1)} %copy-done.16), kind=kOutput, calls=%fused_computation.224 | convolution fusion | flops 119276416 | bytes 2312192 | tf_op jit(solution)/shard_map/sub | solution.py:44
  80.7 2.1 %fusion.207 = (f32[128,4]{0,1:T(4,128)S(1)}, f32[128,4,896]{2,0,1:T(8,128)}) fusion(pred[128,896]{1,0:T(8,128)(4,1)S(1)} %compare_and_fusion, bf16[16,4,8,128]{3,2,1,0:T(8,128)(2,1)S(1)} %get-tuple-element.13, bf16[896,512]{1,0:T(8,128)(2,1)S(1)} %copy-done.16), kind=kOutput, calls=%fused_computation.223 | convolution fusion | flops 119276416 | bytes 2312192 | tf_op jit(solution)/shard_map/sub | solution.py:44
  83.3 3.4 %fusion.9 = f32[128,4,896]{2,0,1:T(8,128)} fusion(bf16[128,4,128]{0,2,1:T(8,128)(2,1)S(1)} %bitcast.328, bf16[896,512]{1,0:T(8,128)(2,1)S(1)} %constant_dynamic-update-slice_fusion.8, f32[128,4,896]{2,0,1:T(8,128)} %get-tuple-element.35, f32[128,4]{0,1:T(4,128)S(1)} %get-tuple-element.34), kind=kOutput, calls=%fused_computation.9 | convolution fusion | flops 118359424 | bytes 4032512 | tf_op jit(solution)/shard_map/sub | solution.py:48
  86.6 5.7 %multiply_reduce_fusion.6 = (f32[128,4]{0,1:T(4,128)S(1)}, f32[128,4,896]{2,0,1:T(8,128)}) fusion(f32[128,4,896]{2,0,1:T(8,128)} %get-tuple-element.35, f32[128,4]{0,1:T(4,128)S(1)} %get-tuple-element.34, f32[128,4,896]{2,0,1:T(8,128)} %fusion.9, f32[896,128,4]{0,1,2:T(8,128)} %fusion.75, bf16[16,4,8,128]{3,2,1,0:T(8,128)(2,1)} %get-tuple-element.8, ...), kind=kOutput, calls=%fused_computation.47 | convolution fusion | flops 239469440 | bytes 9902080 | tf_op jit(solution)/shard_map/sub | solution.py:48
  92.3 3.8 %fusion.37 = bf16[128,4,128]{0,2,1:T(8,128)(2,1)} fusion(f32[128,4,896]{2,0,1:T(8,128)} %get-tuple-element.37, f32[128,4]{0,1:T(4,128)S(1)} %get-tuple-element.36, bf16[896,512]{1,0:T(8,128)(2,1)} %copy-done.15, f32[128,4]{0,1:T(4,128)S(1)} %get-tuple-element.34, pred[128,896]{1,0:T(8,128)(4,1)} %copy-done.13, bf16[16,4,8,128]{3,2,1,0:T(8,128)(2,1)} %get-tuple-element.12), kind=kOutput, calls=%fused_computation.64 | convolution fusion | flops 238224768 | bytes 2674688 | tf_op jit(solution)/shard_map/tgk,kd->tgd/dot_general | solution.py:52
  96.2 3.4 %fusion.6 = f32[128,4,896]{2,0,1:T(8,128)} fusion(bf16[128,4,128]{0,2,1:T(8,128)(2,1)S(1)} %bitcast.326, bf16[896,512]{1,0:T(8,128)(2,1)S(1)} %constant_dynamic-update-slice_fusion.8, f32[128,4,896]{2,0,1:T(8,128)} %get-tuple-element.31, f32[128,4]{0,1:T(4,128)S(1)} %get-tuple-element.30), kind=kOutput, calls=%fused_computation.6 | convolution fusion | flops 118359424 | bytes 4032512 | tf_op jit(solution)/shard_map/sub | solution.py:48
  99.5 5.6 %multiply_reduce_fusion.4 = (f32[128,4]{0,1:T(4,128)S(1)}, f32[128,4,896]{2,0,1:T(8,128)}) fusion(f32[128,4,896]{2,0,1:T(8,128)} %get-tuple-element.31, f32[128,4]{0,1:T(4,128)S(1)} %get-tuple-element.30, f32[128,4,896]{2,0,1:T(8,128)} %fusion.6, f32[896,128,4]{0,1,2:T(8,128)} %fusion.74, bf16[16,4,8,128]{3,2,1,0:T(8,128)(2,1)S(1)} %copy-done.12, ...), kind=kOutput, calls=%fused_computation.41 | convolution fusion | flops 239469440 | bytes 9902080 | tf_op jit(solution)/shard_map/sub | solution.py:48
  105.1 3.2 %fusion.38 = bf16[128,4,128]{0,2,1:T(8,128)(2,1)S(1)} fusion(f32[128,4,896]{2,0,1:T(8,128)} %get-tuple-element.33, f32[128,4]{0,1:T(4,128)S(1)} %get-tuple-element.32, bf16[896,512]{1,0:T(8,128)(2,1)} %copy-done.15, f32[128,4]{0,1:T(4,128)S(1)} %get-tuple-element.30, pred[128,896]{1,0:T(8,128)(4,1)} %copy-done.13, bf16[16,4,8,128]{3,2,1,0:T(8,128)(2,1)} %copy-done.9), kind=kOutput, calls=%fused_computation.65 | convolution fusion | flops 238224768 | bytes 2674688 | tf_op jit(solution)/shard_map/tgk,kd->tgd/dot_general | solution.py:52
  108.3 3.4 %fusion.3 = f32[128,4,896]{2,0,1:T(8,128)} fusion(bf16[128,4,128]{0,2,1:T(8,128)(2,1)S(1)} %bitcast.324, bf16[896,512]{1,0:T(8,128)(2,1)S(1)} %constant_dynamic-update-slice_fusion.8, f32[128,4,896]{2,0,1:T(8,128)} %get-tuple-element.27, f32[128,4]{0,1:T(4,128)S(1)} %get-tuple-element.26), kind=kOutput, calls=%fused_computation.3 | convolution fusion | flops 118359424 | bytes 4032512 | tf_op jit(solution)/shard_map/sub | solution.py:48
  111.7 5.8 %multiply_reduce_fusion.2 = (f32[128,4]{0,1:T(4,128)S(1)}, f32[128,4,896]{2,0,1:T(8,128)}) fusion(f32[128,4,896]{2,0,1:T(8,128)} %get-tuple-element.27, f32[128,4]{0,1:T(4,128)S(1)} %get-tuple-element.26, f32[128,4,896]{2,0,1:T(8,128)} %fusion.3, f32[896,128,4]{0,1,2:T(8,128)} %fusion.73, bf16[16,4,8,128]{3,2,1,0:T(8,128)(2,1)S(1)} %copy-done.10, ...), kind=kOutput, calls=%fused_computation.35 | convolution fusion | flops 239469440 | bytes 9902080 | tf_op jit(solution)/shard_map/sub | solution.py:48
  117.6 3.2 %fusion.39 = bf16[128,4,128]{0,2,1:T(8,128)(2,1)S(1)} fusion(f32[128,4,896]{2,0,1:T(8,128)} %get-tuple-element.29, f32[128,4]{0,1:T(4,128)S(1)} %get-tuple-element.28, bf16[896,512]{1,0:T(8,128)(2,1)} %copy-done.15, f32[128,4]{0,1:T(4,128)S(1)} %get-tuple-element.26, pred[128,896]{1,0:T(8,128)(4,1)} %copy-done.13, bf16[16,4,8,128]{3,2,1,0:T(8,128)(2,1)} %copy-done.7), kind=kOutput, calls=%fused_computation.66 | convolution fusion | flops 238224768 | bytes 2674688 | tf_op jit(solution)/shard_map/tgk,kd->tgd/dot_general | solution.py:52
  120.7 3.3 %fusion = f32[128,4,896]{2,0,1:T(8,128)} fusion(bf16[128,4,128]{0,2,1:T(8,128)(2,1)S(1)} %bitcast.322, bf16[896,512]{1,0:T(8,128)(2,1)S(1)} %constant_dynamic-update-slice_fusion.8, f32[128,4,896]{2,0,1:T(8,128)} %get-tuple-element.23, f32[128,4]{0,1:T(4,128)S(1)} %get-tuple-element.22), kind=kOutput, calls=%fused_computation | convolution fusion | flops 118359424 | bytes 4032512 | tf_op jit(solution)/shard_map/sub | solution.py:48
  124.1 5.1 %multiply_reduce_fusion = (f32[128,4]{0,1:T(4,128)S(1)}, f32[128,4,896]{2,0,1:T(8,128)}) fusion(f32[128,4,896]{2,0,1:T(8,128)} %get-tuple-element.23, f32[128,4]{0,1:T(4,128)S(1)} %get-tuple-element.22, f32[128,4,896]{2,0,1:T(8,128)} %fusion, f32[896,128,4]{0,1,2:T(8,128)S(1)} %fusion.72, bf16[16,4,8,128]{3,2,1,0:T(8,128)(2,1)S(1)} %copy-done.8, ...), kind=kOutput, calls=%fused_computation.29 | convolution fusion | flops 239469440 | bytes 9902080 | tf_op jit(solution)/shard_map/sub | solution.py:48
  129.2 3.2 %fusion.40 = bf16[128,4,128]{0,2,1:T(8,128)(2,1)S(1)} fusion(f32[128,4,896]{2,0,1:T(8,128)} %get-tuple-element.25, f32[128,4]{0,1:T(4,128)S(1)} %get-tuple-element.24, bf16[896,512]{1,0:T(8,128)(2,1)S(1)} %copy-done.17, f32[128,4]{0,1:T(4,128)S(1)} %get-tuple-element.22, pred[128,896]{1,0:T(8,128)(4,1)} %copy-done.13, bf16[16,4,8,128]{3,2,1,0:T(8,128)(2,1)} %copy-done.6), kind=kOutput, calls=%fused_computation.67 | convolution fusion | flops 238224768 | bytes 2674688 | tf_op jit(solution)/shard_map/tgk,kd->tgd/dot_general | solution.py:52
  134.8 42.3 %all-gather.3.cloned.1.call-done = f32[16,1,32768]{2,1,0:T(1,128)} async-done(((f32[1,1,32768]{2,1,0:T(1,128)}), f32[16,1,32768]{2,1,0:T(1,128)}) %all-gather.3.cloned.1.call-update) | async-done | bytes 2097168 | tf_op jit(solution)/shard_map/all_gather | solution.py:113
  177.0 3.0 %reduce_sum.197 = f32[32768]{0:T(1024)S(1)} reduce(f32[16,1,32768]{2,1,0:T(1,128)} %all-gather.3.cloned.1.call-done, f32[]{:T(128)} %constant.6.clone.1), dimensions={0,1}, to_apply=%region_21.22 | reduce | flops 491520 | bytes 2228228 | tf_op jit(solution)/shard_map/reduce_sum | solution.py:113
  184.7 5.0 %psum.7 = f32[2048]{0:T(1024)S(1)} all-reduce(f32[2048]{0:T(1024)S(1)} %bitcast.341), channel_id=1, replica_groups=mesh['task'=2,'ctx'=16] {'task'}, use_global_device_ids=true, to_apply=%region_24.25 | all-reduce | flops 2048 | bytes 16384 | tf_op jit(solution)/shard_map/psum | solution.py:121
  (114 shorter events, 25.4 us)
Async XLA Ops:
  7.2 14.6 %copy-start = (bf16[1,16,2048]{2,1,0:T(8,128)(2,1)S(1)}, bf16[1,16,2048]{2,1,0:T(8,128)(2,1)}, u32[]{:S(2)}) copy-start(bf16[1,16,2048]{2,1,0:T(8,128)(2,1)} %param.13) | copy-start | bytes 196612
  7.2 16.7 %copy-start.3 = (bf16[1,128,2048]{2,1,0:T(8,128)(2,1)S(1)}, bf16[1,128,2048]{2,1,0:T(8,128)(2,1)}, u32[]{:S(2)}) copy-start(bf16[1,128,2048]{2,1,0:T(8,128)(2,1)} %param.16) | copy-start | bytes 1572868
  7.2 169.8 %all-gather.3.cloned.1.call-start = ((), (), s32[]{:S(2)}) async-start(), calls=%async_computation | async-start | bytes 2228224 | tf_op jit(solution)/shard_map/all_gather | solution.py:113
  7.2 19.9 %collective-permute-start = (s32[128]{0:T(128)}, s32[128]{0:T(128)S(1)}, u32[]{:S(2)}, u32[]{:S(2)}) collective-permute-start(s32[128]{0:T(128)} %bitcast.345), channel_id=1, source_target_pairs={{0,6},{1,7},{2,8},{3,9},{4,10},{5,11},{6,12},{7,13},{8,14},{9,15},... | collective-permute-start | bytes 1544 | tf_op jit(solution)/shard_map/ppermute | solution.py:16
  11.8 17.3 %collective-permute-start.1 = (s32[128]{0:T(128)}, s32[128]{0:T(128)S(1)}, u32[]{:S(2)}, u32[]{:S(2)}) collective-permute-start(s32[128]{0:T(128)} %bitcast.346), channel_id=1, source_target_pairs={{0,5},{1,6},{2,7},{3,8},{4,9},{5,10},{6,11},{7,12},{8,13},{9,14},{... | collective-permute-start | bytes 1544 | tf_op jit(solution)/shard_map/ppermute | solution.py:16
  14.5 16.0 %collective-permute-start.2 = (s32[128]{0:T(128)}, s32[128]{0:T(128)S(1)}, u32[]{:S(2)}, u32[]{:S(2)}) collective-permute-start(s32[128]{0:T(128)} %bitcast.347), channel_id=1, source_target_pairs={{0,4},{1,5},{2,6},{3,7},{4,8},{5,9},{6,10},{7,11},{8,12},{9,13},{1... | collective-permute-start | bytes 1544 | tf_op jit(solution)/shard_map/ppermute | solution.py:16
  17.2 14.5 %collective-permute-start.3 = (s32[128]{0:T(128)}, s32[128]{0:T(128)S(1)}, u32[]{:S(2)}, u32[]{:S(2)}) collective-permute-start(s32[128]{0:T(128)} %bitcast.348), channel_id=1, source_target_pairs={{0,3},{1,4},{2,5},{3,6},{4,7},{5,8},{6,9},{7,10},{8,11},{9,12},{10... | collective-permute-start | bytes 1544 | tf_op jit(solution)/shard_map/ppermute | solution.py:16
  19.2 15.2 %collective-permute-start.4 = (s32[128]{0:T(128)}, s32[128]{0:T(128)S(1)}, u32[]{:S(2)}, u32[]{:S(2)}) collective-permute-start(s32[128]{0:T(128)} %bitcast.349), channel_id=1, source_target_pairs={{0,2},{1,3},{2,4},{3,5},{4,6},{5,7},{6,8},{7,9},{8,10},{9,11},{10,... | collective-permute-start | bytes 1544 | tf_op jit(solution)/shard_map/ppermute | solution.py:16
  23.8 47.6 %copy-start.9 = (bf16[16,4,8,128]{3,2,1,0:T(8,128)(2,1)}, bf16[16,4,8,128]{3,2,1,0:T(8,128)(2,1)S(1)}, u32[]{:S(2)}) copy-start(bf16[16,4,8,128]{3,2,1,0:T(8,128)(2,1)S(1)} %get-tuple-element.15) | copy-start | bytes 393220
  23.8 53.1 %copy-start.7 = (bf16[16,4,8,128]{3,2,1,0:T(8,128)(2,1)}, bf16[16,4,8,128]{3,2,1,0:T(8,128)(2,1)S(1)}, u32[]{:S(2)}) copy-start(bf16[16,4,8,128]{3,2,1,0:T(8,128)(2,1)S(1)} %get-tuple-element.14) | copy-start | bytes 393220
  23.8 56.9 %copy-start.6 = (bf16[16,4,8,128]{3,2,1,0:T(8,128)(2,1)}, bf16[16,4,8,128]{3,2,1,0:T(8,128)(2,1)S(1)}, u32[]{:S(2)}) copy-start(bf16[16,4,8,128]{3,2,1,0:T(8,128)(2,1)S(1)} %get-tuple-element.13) | copy-start | bytes 393220
  24.1 5.0 %copy-start.4 = (bf16[1,128,512]{2,1,0:T(8,128)(2,1)S(1)}, bf16[1,128,512]{2,1,0:T(8,128)(2,1)}, u32[]{:S(2)}) copy-start(bf16[1,128,512]{2,1,0:T(8,128)(2,1)} %param.14) | copy-start | bytes 393220
  24.1 17.9 %copy-start.5 = (bf16[1,128,512]{2,1,0:T(8,128)(2,1)S(1)}, bf16[1,128,512]{2,1,0:T(8,128)(2,1)}, u32[]{:S(2)}) copy-start(bf16[1,128,512]{2,1,0:T(8,128)(2,1)} %param.15) | copy-start | bytes 393220
  27.2 10.3 %collective-permute-start.5 = (s32[128]{0:T(128)S(1)}, s32[128]{0:T(128)S(1)}, u32[]{:S(2)}, u32[]{:S(2)}) collective-permute-start(s32[128]{0:T(128)S(1)} %bitcast.350), channel_id=1, source_target_pairs={{0,1},{1,2},{2,3},{3,4},{4,5},{5,6},{6,7},{7,8},{8,9},{9,10},{10,1... | collective-permute-start | bytes 1544 | tf_op jit(solution)/shard_map/ppermute | solution.py:16
  29.1 10.8 %collective-permute-start.6 = (bf16[128,512]{1,0:T(8,128)(2,1)S(1)}, bf16[128,512]{1,0:T(8,128)(2,1)S(1)}, u32[]{:S(2)}, u32[]{:S(2)}) collective-permute-start(bf16[128,512]{1,0:T(8,128)(2,1)S(1)} %bitcast.329), channel_id=1, source_target_pairs={{0,6},{1,7},{2,8},{3,9},{4,10},{5,11},{6,12},{7,13},{8,14},{9,15},... | collective-permute-start | bytes 393224 | tf_op jit(solution)/shard_map/ppermute | solution.py:16
  30.5 11.6 %collective-permute-start.7 = (bf16[128,512]{1,0:T(8,128)(2,1)S(1)}, bf16[128,512]{1,0:T(8,128)(2,1)S(1)}, u32[]{:S(2)}, u32[]{:S(2)}) collective-permute-start(bf16[128,512]{1,0:T(8,128)(2,1)S(1)} %bitcast.330), channel_id=1, source_target_pairs={{0,5},{1,6},{2,7},{3,8},{4,9},{5,10},{6,11},{7,12},{8,13},{9,14},{... | collective-permute-start | bytes 393224 | tf_op jit(solution)/shard_map/ppermute | solution.py:16
  31.8 11.6 %collective-permute-start.8 = (bf16[128,512]{1,0:T(8,128)(2,1)S(1)}, bf16[128,512]{1,0:T(8,128)(2,1)S(1)}, u32[]{:S(2)}, u32[]{:S(2)}) collective-permute-start(bf16[128,512]{1,0:T(8,128)(2,1)S(1)} %bitcast.331), channel_id=1, source_target_pairs={{0,4},{1,5},{2,6},{3,7},{4,8},{5,9},{6,10},{7,11},{8,12},{9,13},{1... | collective-permute-start | bytes 393224 | tf_op jit(solution)/shard_map/ppermute | solution.py:16
  34.4 10.3 %collective-permute-start.9 = (bf16[128,512]{1,0:T(8,128)(2,1)S(1)}, bf16[128,512]{1,0:T(8,128)(2,1)S(1)}, u32[]{:S(2)}, u32[]{:S(2)}) collective-permute-start(bf16[128,512]{1,0:T(8,128)(2,1)S(1)} %bitcast.332), channel_id=1, source_target_pairs={{0,3},{1,4},{2,5},{3,6},{4,7},{5,8},{6,9},{7,10},{8,11},{9,12},{10... | collective-permute-start | bytes 393224 | tf_op jit(solution)/shard_map/ppermute | solution.py:16
  37.5 11.1 %collective-permute-start.10 = (bf16[128,512]{1,0:T(8,128)(2,1)S(1)}, bf16[128,512]{1,0:T(8,128)(2,1)S(1)}, u32[]{:S(2)}, u32[]{:S(2)}) collective-permute-start(bf16[128,512]{1,0:T(8,128)(2,1)S(1)} %bitcast.333), channel_id=1, source_target_pairs={{0,2},{1,3},{2,4},{3,5},{4,6},{5,7},{6,8},{7,9},{8,10},{9,11},{10,... | collective-permute-start | bytes 393224 | tf_op jit(solution)/shard_map/ppermute | solution.py:16
  39.9 40.8 %copy-start.13 = (pred[128,896]{1,0:T(8,128)(4,1)}, pred[128,896]{1,0:T(8,128)(4,1)S(1)}, u32[]{:S(2)}) copy-start(pred[128,896]{1,0:T(8,128)(4,1)S(1)} %compare_and_fusion) | copy-start | bytes 344068
  39.9 28.3 %copy-start.11 = (bf16[16,4,8,128]{3,2,1,0:T(8,128)(2,1)S(1)}, bf16[16,4,8,128]{3,2,1,0:T(8,128)(2,1)}, u32[]{:S(2)}) copy-start(bf16[16,4,8,128]{3,2,1,0:T(8,128)(2,1)} %get-tuple-element.12) | copy-start | bytes 393220
  40.0 13.6 %collective-permute-start.11 = (bf16[128,512]{1,0:T(8,128)(2,1)S(1)}, bf16[128,512]{1,0:T(8,128)(2,1)S(1)}, u32[]{:S(2)}, u32[]{:S(2)}) collective-permute-start(bf16[128,512]{1,0:T(8,128)(2,1)S(1)} %bitcast.334), channel_id=1, source_target_pairs={{0,1},{1,2},{2,3},{3,4},{4,5},{5,6},{6,7},{7,8},{8,9},{9,10},{10,1... | collective-permute-start | bytes 393224 | tf_op jit(solution)/shard_map/ppermute | solution.py:16
  42.1 17.3 %collective-permute-start.12 = (bf16[128,512]{1,0:T(8,128)(2,1)S(1)}, bf16[128,512]{1,0:T(8,128)(2,1)S(1)}, u32[]{:S(2)}, u32[]{:S(2)}) collective-permute-start(bf16[128,512]{1,0:T(8,128)(2,1)S(1)} %bitcast.335), channel_id=1, source_target_pairs={{0,6},{1,7},{2,8},{3,9},{4,10},{5,11},{6,12},{7,13},{8,14},{9,15},... | collective-permute-start | bytes 393224 | tf_op jit(solution)/shard_map/ppermute | solution.py:16
  43.4 20.2 %collective-permute-start.13 = (bf16[128,512]{1,0:T(8,128)(2,1)S(1)}, bf16[128,512]{1,0:T(8,128)(2,1)S(1)}, u32[]{:S(2)}, u32[]{:S(2)}) collective-permute-start(bf16[128,512]{1,0:T(8,128)(2,1)S(1)} %bitcast.336), channel_id=1, source_target_pairs={{0,5},{1,6},{2,7},{3,8},{4,9},{5,10},{6,11},{7,12},{8,13},{9,14},{... | collective-permute-start | bytes 393224 | tf_op jit(solution)/shard_map/ppermute | solution.py:16
  44.7 18.9 %collective-permute-start.14 = (bf16[128,512]{1,0:T(8,128)(2,1)S(1)}, bf16[128,512]{1,0:T(8,128)(2,1)S(1)}, u32[]{:S(2)}, u32[]{:S(2)}) collective-permute-start(bf16[128,512]{1,0:T(8,128)(2,1)S(1)} %bitcast.337), channel_id=1, source_target_pairs={{0,4},{1,5},{2,6},{3,7},{4,8},{5,9},{6,10},{7,11},{8,12},{9,13},{1... | collective-permute-start | bytes 393224 | tf_op jit(solution)/shard_map/ppermute | solution.py:16
  48.6 15.0 %collective-permute-start.15 = (bf16[128,512]{1,0:T(8,128)(2,1)S(1)}, bf16[128,512]{1,0:T(8,128)(2,1)S(1)}, u32[]{:S(2)}, u32[]{:S(2)}) collective-permute-start(bf16[128,512]{1,0:T(8,128)(2,1)S(1)} %bitcast.338), channel_id=1, source_target_pairs={{0,3},{1,4},{2,5},{3,6},{4,7},{5,8},{6,9},{7,10},{8,11},{9,12},{10... | collective-permute-start | bytes 393224 | tf_op jit(solution)/shard_map/ppermute | solution.py:16
  53.6 10.1 %collective-permute-start.16 = (bf16[128,512]{1,0:T(8,128)(2,1)S(1)}, bf16[128,512]{1,0:T(8,128)(2,1)S(1)}, u32[]{:S(2)}, u32[]{:S(2)}) collective-permute-start(bf16[128,512]{1,0:T(8,128)(2,1)S(1)} %bitcast.339), channel_id=1, source_target_pairs={{0,2},{1,3},{2,4},{3,5},{4,6},{5,7},{6,8},{7,9},{8,10},{9,11},{10,... | collective-permute-start | bytes 393224 | tf_op jit(solution)/shard_map/ppermute | solution.py:16
  59.4 8.9 %copy-start.15 = (bf16[896,512]{1,0:T(8,128)(2,1)}, bf16[896,512]{1,0:T(8,128)(2,1)S(1)}, u32[]{:S(2)}) copy-start(bf16[896,512]{1,0:T(8,128)(2,1)S(1)} %constant_dynamic-update-slice_fusion.1) | copy-start | bytes 2752516
  59.4 8.8 %collective-permute-start.17 = (bf16[128,512]{1,0:T(8,128)(2,1)S(1)}, bf16[128,512]{1,0:T(8,128)(2,1)S(1)}, u32[]{:S(2)}, u32[]{:S(2)}) collective-permute-start(bf16[128,512]{1,0:T(8,128)(2,1)S(1)} %bitcast.340), channel_id=1, source_target_pairs={{0,1},{1,2},{2,3},{3,4},{4,5},{5,6},{6,7},{7,8},{8,9},{9,10},{10,1... | collective-permute-start | bytes 393224 | tf_op jit(solution)/shard_map/ppermute | solution.py:16
  108.3 3.4 %copy-start.10 = (bf16[16,4,8,128]{3,2,1,0:T(8,128)(2,1)S(1)}, bf16[16,4,8,128]{3,2,1,0:T(8,128)(2,1)}, u32[]{:S(2)}) copy-start(bf16[16,4,8,128]{3,2,1,0:T(8,128)(2,1)} %get-tuple-element.10) | copy-start | bytes 393220
  124.1 5.1 %copy-start.17 = (bf16[896,512]{1,0:T(8,128)(2,1)S(1)}, bf16[896,512]{1,0:T(8,128)(2,1)}, u32[]{:S(2)}) copy-start(bf16[896,512]{1,0:T(8,128)(2,1)} %copy-done.15) | copy-start | bytes 2752516
  184.7 6.2 %copy-start.14 = (f32[1,2048]{1,0:T(1,128)}, f32[1,2048]{1,0:T(1,128)S(1)}, u32[]{:S(2)}) copy-start(f32[1,2048]{1,0:T(1,128)S(1)} %get-tuple-element.21) | copy-start | bytes 24580
  (8 other events, 22.0 us)
Sparse Core Ops, SparseCore 0:
  133.6 43.4 all-gather.2
